TPU v7x, 32 devices: a whole 2x2x4 slice. The times are simulated.
32 devices in a mesh: seq: 8 (over y, x, core), kvh: 4 (over z).
Axes of the slice: x: 2, y: 2, z: 4, core: 2. Of those that a mesh axis runs over, the one named last changes fastest.
Arguments:
- queries: bfloat16 [64, 32, 128], P(('seq', 'kvh')), may hold values from -9 to 9
- attn_out: bfloat16 [64, 32, 128], P(('seq', 'kvh')), may hold values from -0.59765625 to 0.59765625
- grad_out: bfloat16 [64, 32, 128], P(('seq', 'kvh')), may hold values from -384 to 384
- log_norms: float32 [64, 32], P(('seq', 'kvh')), may hold values from 0 to 14, as said below
- query_starts: int32 [64], replicated, may hold values from 0 to 2048
- keys: bfloat16 [8192, 4, 128], P('seq', 'kvh'), may hold values from -6 to 6
- values: bfloat16 [8192, 4, 128], P('seq', 'kvh'), may hold values from -6 to 6
Outputs:
- grad_query: bfloat16 [64, 32, 128], P(('seq', 'kvh'))
- grad_keys: bfloat16 [8192, 4, 128], P('seq', 'kvh')
- grad_values: bfloat16 [8192, 4, 128], P('seq', 'kvh')
Inputs may be any that keep to these rules, and one draw needn't show every extreme that they name: `log_norms`: each entry lies within one of the log of its token's number of visible positions plus 1.125.
All inputs are finite; a program needn't handle non-finite values.
Results may differ from a plain program's by a relative error of at most 0.0052.
Values may be sent and summed in bfloat16 or wider, within the bound.
No kernel may reach another device: no remote copies, remote signals or barrier semaphores. Data moves between devices by JAX's collectives and lax.ppermute only.
A program may use at most 64 MiB of HBM per device.

v0:
```python
import jax
import jax.numpy as jnp
from jax import lax
from jax.sharding import PartitionSpec as P


def shifted(value, axis, by):
    peers = lax.axis_size(axis)
    return lax.ppermute(value, axis, [(i, (i + by) % peers) for i in range(peers)])


def local(queries, attn_out, grad_out, log_norms, query_starts, keys, values):
    scaling = queries.shape[-1] ** (-0.5)
    seq_count = lax.axis_size("seq")
    seq_index = lax.axis_index("seq")
    deltas = jnp.sum(grad_out.astype(jnp.float32) * attn_out.astype(jnp.float32), axis=-1)
    query_block, grad_block = (
        lax.all_to_all(queries, "kvh", split_axis=1, concat_axis=0, tiled=True),
        lax.all_to_all(grad_out, "kvh", split_axis=1, concat_axis=0, tiled=True),
    )
    norm_block, delta_block = (
        lax.all_to_all(log_norms, "kvh", split_axis=1, concat_axis=0, tiled=True),
        lax.all_to_all(deltas, "kvh", split_axis=1, concat_axis=0, tiled=True),
    )
    block_rows = query_block.shape[0]
    total_rows = block_rows * seq_count
    key_count = keys.shape[0]
    key_rows = keys[:, 0, :]
    value_rows = values[:, 0, :]
    key_pos = seq_index * key_count + jnp.arange(key_count, dtype=jnp.int32)
    offset = key_count * seq_count - total_rows

    def block_terms(queries_in, grads_in, norms_in, deltas_in, first_row):
        row_count = queries_in.shape[0]
        query_pos = offset + first_row + jnp.arange(row_count, dtype=jnp.int32)
        first_keys = lax.dynamic_slice_in_dim(query_starts, first_row, row_count)
        visible = (key_pos[None, :] >= first_keys[:, None]) & (
            key_pos[None, :] <= query_pos[:, None]
        )
        scores = (
            jnp.einsum("rgd,kd->rgk", queries_in, key_rows, preferred_element_type=jnp.float32)
            * scaling
        )
        weights = jnp.where(visible[:, None, :], jnp.exp(scores - norms_in[..., None]), 0.0)
        weight_grad = jnp.einsum(
            "rgd,kd->rgk", grads_in, value_rows, preferred_element_type=jnp.float32
        )
        score_grad = weights * (weight_grad - deltas_in[..., None])
        weight_half = weights.astype(jnp.bfloat16)
        score_half = score_grad.astype(jnp.bfloat16)
        value_part = jnp.einsum(
            "rgk,rgd->kd", weight_half, grads_in, preferred_element_type=jnp.float32
        )
        key_part = (
            jnp.einsum("rgk,rgd->kd", score_half, queries_in, preferred_element_type=jnp.float32)
            * scaling
        )
        query_part = (
            jnp.einsum("rgk,kd->rgd", score_half, key_rows, preferred_element_type=jnp.float32)
            * scaling
        )
        return (key_part, value_part, query_part)

    key_empty = jnp.zeros(key_rows.shape, jnp.float32)

    def visit_owner(counter, carried):
        query_now, grad_now, norm_now, delta_now, query_grad, key_grad, value_grad = carried
        anchor = (seq_index - counter) % seq_count
        key_part, value_part, query_part = block_terms(
            query_now, grad_now, norm_now, delta_now, anchor * block_rows
        )
        query_now, grad_now = shifted((query_now, grad_now), "seq", 1)
        norm_now, delta_now, query_grad = shifted(
            (norm_now, delta_now, query_grad + query_part), "seq", 1
        )
        return (
            query_now,
            grad_now,
            norm_now,
            delta_now,
            query_grad,
            key_grad + key_part,
            value_grad + value_part,
        )

    query_empty = jnp.zeros(query_block.shape, jnp.float32)
    carried = (query_block, grad_block, norm_block, delta_block, query_empty, key_empty, key_empty)
    carried = lax.fori_loop(0, seq_count - 1, visit_owner, carried)
    query_now, grad_now, norm_now, delta_now, query_grad, key_grad, value_grad = carried
    anchor = (seq_index + 1) % seq_count
    key_part, value_part, query_part = block_terms(
        query_now, grad_now, norm_now, delta_now, anchor * block_rows
    )
    key_grad = key_grad + key_part
    value_grad = value_grad + value_part
    query_grad = shifted((query_grad + query_part).astype(jnp.bfloat16), "seq", 1).astype(
        jnp.float32
    )
    grad_query = lax.all_to_all(
        query_grad.astype(jnp.bfloat16), "kvh", split_axis=0, concat_axis=1, tiled=True
    )
    return (
        grad_query,
        key_grad.astype(jnp.bfloat16)[:, None, :],
        value_grad.astype(jnp.bfloat16)[:, None, :],
    )


def solution(mesh):
    return jax.shard_map(
        local,
        mesh=mesh,
        in_specs=(
            P(("seq", "kvh"), None, None),
            P(("seq", "kvh"), None, None),
            P(("seq", "kvh"), None, None),
            P(("seq", "kvh"), None),
            P(),
            P("seq", "kvh", None),
            P("seq", "kvh", None),
        ),
        out_specs=(P(("seq", "kvh"), None, None), P("seq", "kvh", None), P("seq", "kvh", None)),
        check_vma=False,
    )
```

profile of v0, /device:TPU:0, one launch (start us, length us, event | category | flops | bytes accessed | tf_op | source)
XLA Modules:
  0.0 116.3 jit_solution(9681202412714350968)
XLA Ops:
  0.7 0.8 all_to_all.75
  1.5 0.6 copy.31
  2.1 6.3 %all-to-all-start.2 = ((f32[2,4,8]{2,0,1:T(2,128)}), f32[2,4,8]{2,0,1:T(2,128)S(1)}, u32[]{:S(2)}, u32[]{:S(2)}) async-start(f32[2,4,8]{2,0,1:T(2,128)} %copy.31), calls=%async_computation.2 | async-start | bytes 8192 | tf_op jit(solution)/shard_map/all_to_all | solution.py:22
  8.4 0.6 copy.27
  9.0 0.7 dynamic_slice.13
  9.8 4.2 %all-to-all-done.2 = f32[2,4,8]{2,0,1:T(2,128)S(1)} async-done(((f32[2,4,8]{2,0,1:T(2,128)}), f32[2,4,8]{2,0,1:T(2,128)S(1)}, u32[]{:S(2)}, u32[]{:S(2)}) %all-to-all-start.2) | async-done | bytes 288 | tf_op jit(solution)/shard_map/all_to_all | solution.py:22
  14.0 3.3 %all-to-all-start = ((bf16[2,32,128]{2,0,1:T(2,128)(2,1)}), bf16[2,32,128]{2,0,1:T(2,128)(2,1)S(1)}, u32[]{:S(2)}, u32[]{:S(2)}) async-start(bf16[2,32,128]{2,0,1:T(2,128)(2,1)} %copy.27), calls=%async_computation | async-start | bytes 32768 | tf_op jit(solution)/shard_map/all_to_all | solution.py:18
  17.3 1.3 %copy.29 = bf16[2,32,128]{2,0,1:T(2,128)(2,1)} copy(bf16[2,32,128]{2,1,0:T(8,128)(2,1)} %param.11) | data formatting | bytes 32768 | tf_op args[2]
  18.7 4.2 %all-to-all-done = bf16[2,32,128]{2,0,1:T(2,128)(2,1)S(1)} async-done(((bf16[2,32,128]{2,0,1:T(2,128)(2,1)}), bf16[2,32,128]{2,0,1:T(2,128)(2,1)S(1)}, u32[]{:S(2)}, u32[]{:S(2)}) %all-to-all-start) | async-done | bytes 16416 | tf_op jit(solution)/shard_map/all_to_all | solution.py:18
  22.8 3.3 %all-to-all-start.1 = ((bf16[2,32,128]{2,0,1:T(2,128)(2,1)}), bf16[2,32,128]{2,0,1:T(2,128)(2,1)S(1)}, u32[]{:S(2)}, u32[]{:S(2)}) async-start(bf16[2,32,128]{2,0,1:T(2,128)(2,1)} %copy.29), calls=%async_computation.1 | async-start | bytes 32768 | tf_op jit(solution)/shard_map/all_to_all | solution.py:19
  26.1 0.8 multiply_reduce_fusion
  27.0 0.6 copy.32
  27.6 4.1 %all-to-all-done.1 = bf16[2,32,128]{2,0,1:T(2,128)(2,1)S(1)} async-done(((bf16[2,32,128]{2,0,1:T(2,128)(2,1)}), bf16[2,32,128]{2,0,1:T(2,128)(2,1)S(1)}, u32[]{:S(2)}, u32[]{:S(2)}) %all-to-all-start.1) | async-done | bytes 16416 | tf_op jit(solution)/shard_map/all_to_all | solution.py:19
  31.7 3.2 %all-to-all-start.3 = ((f32[2,4,8]{2,0,1:T(2,128)}), f32[2,4,8]{2,0,1:T(2,128)S(1)}, u32[]{:S(2)}, u32[]{:S(2)}) async-start(f32[2,4,8]{2,0,1:T(2,128)} %copy.32), calls=%async_computation.3 | async-start | bytes 8192 | tf_op jit(solution)/shard_map/all_to_all | solution.py:23
  35.0 5.5 %all-to-all-done.3 = f32[2,4,8]{2,0,1:T(2,128)S(1)} async-done(((f32[2,4,8]{2,0,1:T(2,128)}), f32[2,4,8]{2,0,1:T(2,128)S(1)}, u32[]{:S(2)}, u32[]{:S(2)}) %all-to-all-start.3) | async-done | bytes 288 | tf_op jit(solution)/shard_map/all_to_all | solution.py:23
  40.5 0.6 copy-done.4
  41.1 60.2 %while.28 = (s32[]{:T(128)}, bf16[8,8,128]{2,0,1:T(8,128)(2,1)S(1)}, bf16[8,8,128]{2,0,1:T(8,128)(2,1)S(1)}, f32[8,8]{1,0:T(8,128)S(1)}, f32[8,8]{1,0:T(8,128)S(...) while((s32[]{:T(128)}, ...), condition=%wide.region_2.3_spmd.clone, body=%wide.region_1.2_spmd.clone.sunk | while | flops 85042200 | bytes 5599483 | solution.py:88
  41.1 1.6 %collective-permute-start.1 = (bf16[8,8,128]{2,0,1:T(8,128)(2,1)S(1)}, bf16[8,8,128]{2,0,1:T(8,128)(2,1)S(1)}, u32[]{:S(2)}, u32[]{:S(2)}) collective-permute-start(bf16[8,8,128]{2,0,1:T(8,128)(2,1)S(1)} %copy.78), channel_id=1, source_target_pairs={{0,4},{4,8},{8,12},{12,16},{16,20},{20,24},{24,28},{28,0},{1,5},{5... | collective-permute-start | bytes 49160 | tf_op jit(solution)/shard_map/while/body/eval_jaxpr/ppermute | solution.py:9
  42.8 1.5 %collective-permute-start.3 = (f32[8,8]{1,0:T(8,128)S(1)}, f32[8,8]{1,0:T(8,128)S(1)}, u32[]{:S(2)}, u32[]{:S(2)}) collective-permute-start(f32[8,8]{1,0:T(8,128)S(1)} %copy.80), channel_id=1, source_target_pairs={{0,4},{4,8},{8,12},{12,16},{16,20},{20,24},{24,28},{28,0},{1,5},{5... | collective-permute-start | bytes 776 | tf_op jit(solution)/shard_map/while/body/eval_jaxpr/ppermute | solution.py:9
  44.7 0.7 copy-done.1
  46.3 0.3 fusion.73
  46.7 3.4 %collective-permute-done.4 = f32[8,8,128]{2,1,0:T(8,128)S(1)} collective-permute-done((f32[8,8,128]{2,1,0:T(8,128)S(1)}, f32[8,8,128]{2,1,0:T(8,128)S(1)}, u32[]{:S(2)}, u32[]{:S(2)}) %collective-permute-start.4) | collective-permute-done | bytes 32800 | tf_op jit(solution)/shard_map/while/body/eval_jaxpr/ppermute | solution.py:9
  50.2 0.7 collective-permute-start.1
  50.9 1.4 %collective-permute-start.3 = (f32[8,8]{1,0:T(8,128)S(1)}, f32[8,8]{1,0:T(8,128)S(1)}, u32[]{:S(2)}, u32[]{:S(2)}) collective-permute-start(f32[8,8]{1,0:T(8,128)S(1)} %copy.80), channel_id=1, source_target_pairs={{0,4},{4,8},{8,12},{12,16},{16,20},{20,24},{24,28},{28,0},{1,5},{5... | collective-permute-start | bytes 776 | tf_op jit(solution)/shard_map/while/body/eval_jaxpr/ppermute | solution.py:9
  52.8 0.7 copy-done.1
  54.9 3.3 %collective-permute-done.4 = f32[8,8,128]{2,1,0:T(8,128)S(1)} collective-permute-done((f32[8,8,128]{2,1,0:T(8,128)S(1)}, f32[8,8,128]{2,1,0:T(8,128)S(1)}, u32[]{:S(2)}, u32[]{:S(2)}) %collective-permute-start.4) | collective-permute-done | bytes 32800 | tf_op jit(solution)/shard_map/while/body/eval_jaxpr/ppermute | solution.py:9
  58.3 3.1 %collective-permute-start.3 = (f32[8,8]{1,0:T(8,128)S(1)}, f32[8,8]{1,0:T(8,128)S(1)}, u32[]{:S(2)}, u32[]{:S(2)}) collective-permute-start(f32[8,8]{1,0:T(8,128)S(1)} %copy.80), channel_id=1, source_target_pairs={{0,4},{4,8},{8,12},{12,16},{16,20},{20,24},{24,28},{28,0},{1,5},{5... | collective-permute-start | bytes 776 | tf_op jit(solution)/shard_map/while/body/eval_jaxpr/ppermute | solution.py:9
  61.8 0.7 copy-done.1
  63.7 3.5 %collective-permute-done.4 = f32[8,8,128]{2,1,0:T(8,128)S(1)} collective-permute-done((f32[8,8,128]{2,1,0:T(8,128)S(1)}, f32[8,8,128]{2,1,0:T(8,128)S(1)}, u32[]{:S(2)}, u32[]{:S(2)}) %collective-permute-start.4) | collective-permute-done | bytes 32800 | tf_op jit(solution)/shard_map/while/body/eval_jaxpr/ppermute | solution.py:9
  67.4 2.0 %collective-permute-start.3 = (f32[8,8]{1,0:T(8,128)S(1)}, f32[8,8]{1,0:T(8,128)S(1)}, u32[]{:S(2)}, u32[]{:S(2)}) collective-permute-start(f32[8,8]{1,0:T(8,128)S(1)} %copy.80), channel_id=1, source_target_pairs={{0,4},{4,8},{8,12},{12,16},{16,20},{20,24},{24,28},{28,0},{1,5},{5... | collective-permute-start | bytes 776 | tf_op jit(solution)/shard_map/while/body/eval_jaxpr/ppermute | solution.py:9
  69.8 0.7 copy-done.1
  71.8 3.5 %collective-permute-done.4 = f32[8,8,128]{2,1,0:T(8,128)S(1)} collective-permute-done((f32[8,8,128]{2,1,0:T(8,128)S(1)}, f32[8,8,128]{2,1,0:T(8,128)S(1)}, u32[]{:S(2)}, u32[]{:S(2)}) %collective-permute-start.4) | collective-permute-done | bytes 32800 | tf_op jit(solution)/shard_map/while/body/eval_jaxpr/ppermute | solution.py:9
  75.4 3.1 %collective-permute-start.3 = (f32[8,8]{1,0:T(8,128)S(1)}, f32[8,8]{1,0:T(8,128)S(1)}, u32[]{:S(2)}, u32[]{:S(2)}) collective-permute-start(f32[8,8]{1,0:T(8,128)S(1)} %copy.80), channel_id=1, source_target_pairs={{0,4},{4,8},{8,12},{12,16},{16,20},{20,24},{24,28},{28,0},{1,5},{5... | collective-permute-start | bytes 776 | tf_op jit(solution)/shard_map/while/body/eval_jaxpr/ppermute | solution.py:9
  78.8 0.7 copy-done.1
  80.8 3.5 %collective-permute-done.4 = f32[8,8,128]{2,1,0:T(8,128)S(1)} collective-permute-done((f32[8,8,128]{2,1,0:T(8,128)S(1)}, f32[8,8,128]{2,1,0:T(8,128)S(1)}, u32[]{:S(2)}, u32[]{:S(2)}) %collective-permute-start.4) | collective-permute-done | bytes 32800 | tf_op jit(solution)/shard_map/while/body/eval_jaxpr/ppermute | solution.py:9
  84.4 2.0 %collective-permute-start.3 = (f32[8,8]{1,0:T(8,128)S(1)}, f32[8,8]{1,0:T(8,128)S(1)}, u32[]{:S(2)}, u32[]{:S(2)}) collective-permute-start(f32[8,8]{1,0:T(8,128)S(1)} %copy.80), channel_id=1, source_target_pairs={{0,4},{4,8},{8,12},{12,16},{16,20},{20,24},{24,28},{28,0},{1,5},{5... | collective-permute-start | bytes 776 | tf_op jit(solution)/shard_map/while/body/eval_jaxpr/ppermute | solution.py:9
  86.8 0.7 copy-done.1
  88.8 3.5 %collective-permute-done.4 = f32[8,8,128]{2,1,0:T(8,128)S(1)} collective-permute-done((f32[8,8,128]{2,1,0:T(8,128)S(1)}, f32[8,8,128]{2,1,0:T(8,128)S(1)}, u32[]{:S(2)}, u32[]{:S(2)}) %collective-permute-start.4) | collective-permute-done | bytes 32800 | tf_op jit(solution)/shard_map/while/body/eval_jaxpr/ppermute | solution.py:9
  92.4 3.1 %collective-permute-start.3 = (f32[8,8]{1,0:T(8,128)S(1)}, f32[8,8]{1,0:T(8,128)S(1)}, u32[]{:S(2)}, u32[]{:S(2)}) collective-permute-start(f32[8,8]{1,0:T(8,128)S(1)} %copy.80), channel_id=1, source_target_pairs={{0,4},{4,8},{8,12},{12,16},{16,20},{20,24},{24,28},{28,0},{1,5},{5... | collective-permute-start | bytes 776 | tf_op jit(solution)/shard_map/while/body/eval_jaxpr/ppermute | solution.py:9
  95.9 0.7 copy-done.1
  97.8 3.5 %collective-permute-done.4 = f32[8,8,128]{2,1,0:T(8,128)S(1)} collective-permute-done((f32[8,8,128]{2,1,0:T(8,128)S(1)}, f32[8,8,128]{2,1,0:T(8,128)S(1)}, u32[]{:S(2)}, u32[]{:S(2)}) %collective-permute-start.4) | collective-permute-done | bytes 32800 | tf_op jit(solution)/shard_map/while/body/eval_jaxpr/ppermute | solution.py:9
  101.5 0.7 copy-done.2
  102.7 1.0 fusion.24
  103.7 3.2 %collective-permute-done.5 = bf16[8,8,128]{2,1,0:T(8,128)(2,1)} collective-permute-done((bf16[8,8,128]{2,1,0:T(8,128)(2,1)S(1)}, bf16[8,8,128]{2,1,0:T(8,128)(2,1)}, u32[]{:S(2)}, u32[]{:S(2)}) %collective-permute-start.5) | collective-permute-done | bytes 16416 | tf_op jit(solution)/shard_map/ppermute | solution.py:9
  106.9 3.2 %all-to-all-start.4 = ((bf16[8,8,128]{2,1,0:T(8,128)(2,1)}), bf16[8,8,128]{2,1,0:T(8,128)(2,1)S(1)}, u32[]{:S(2)}, u32[]{:S(2)}) async-start(bf16[8,8,128]{2,1,0:T(8,128)(2,1)} %collective-permute-done.5), calls=%async_computation.4 | async-start | bytes 32768 | tf_op jit(solution)/shard_map/all_to_all | solution.py:99
  110.1 1.0 fusion.29
  111.1 4.6 %all-to-all-done.4 = bf16[8,8,128]{2,1,0:T(8,128)(2,1)S(1)} async-done(((bf16[8,8,128]{2,1,0:T(8,128)(2,1)}), bf16[8,8,128]{2,1,0:T(8,128)(2,1)S(1)}, u32[]{:S(2)}, u32[]{:S(2)}) %all-to-all-start.4) | async-done | bytes 16416 | tf_op jit(solution)/shard_map/all_to_all | solution.py:99
  115.7 0.6 copy.59
  (170 shorter events, 12.4 us)
Async XLA Ops:
  0.6 7.8 %copy-start.3 = (bf16[2,32,128]{2,1,0:T(8,128)(2,1)S(1)}, bf16[2,32,128]{2,1,0:T(8,128)(2,1)}, u32[]{:S(2)}) copy-start(bf16[2,32,128]{2,1,0:T(8,128)(2,1)} %param.9) | copy-start | bytes 49156
  0.6 39.8 %copy-start = (bf16[1024,1,128]{2,0,1:T(8,128)(2,1)S(1)}, bf16[1024,1,128]{2,0,1:T(8,128)(2,1)}, u32[]{:S(2)}) copy-start(bf16[1024,1,128]{2,0,1:T(8,128)(2,1)} %param.14) | copy-start | bytes 786436
  2.1 11.9 %all-to-all-start.2 = ((f32[2,4,8]{2,0,1:T(2,128)}), f32[2,4,8]{2,0,1:T(2,128)S(1)}, u32[]{:S(2)}, u32[]{:S(2)}) async-start(f32[2,4,8]{2,0,1:T(2,128)} %copy.31), calls=%async_computation.2 | async-start | bytes 8192 | tf_op jit(solution)/shard_map/all_to_all | solution.py:22
  14.0 8.8 %all-to-all-start = ((bf16[2,32,128]{2,0,1:T(2,128)(2,1)}), bf16[2,32,128]{2,0,1:T(2,128)(2,1)S(1)}, u32[]{:S(2)}, u32[]{:S(2)}) async-start(bf16[2,32,128]{2,0,1:T(2,128)(2,1)} %copy.27), calls=%async_computation | async-start | bytes 32768 | tf_op jit(solution)/shard_map/all_to_all | solution.py:18
  22.8 8.8 %all-to-all-start.1 = ((bf16[2,32,128]{2,0,1:T(2,128)(2,1)}), bf16[2,32,128]{2,0,1:T(2,128)(2,1)S(1)}, u32[]{:S(2)}, u32[]{:S(2)}) async-start(bf16[2,32,128]{2,0,1:T(2,128)(2,1)} %copy.29), calls=%async_computation.1 | async-start | bytes 32768 | tf_op jit(solution)/shard_map/all_to_all | solution.py:19
  31.7 8.8 %all-to-all-start.3 = ((f32[2,4,8]{2,0,1:T(2,128)}), f32[2,4,8]{2,0,1:T(2,128)S(1)}, u32[]{:S(2)}, u32[]{:S(2)}) async-start(f32[2,4,8]{2,0,1:T(2,128)} %copy.32), calls=%async_computation.3 | async-start | bytes 8192 | tf_op jit(solution)/shard_map/all_to_all | solution.py:23
  41.1 5.6 %collective-permute-start = (bf16[8,8,128]{2,0,1:T(8,128)(2,1)S(1)}, bf16[8,8,128]{2,0,1:T(8,128)(2,1)S(1)}, u32[]{:S(2)}, u32[]{:S(2)}) collective-permute-start(bf16[8,8,128]{2,0,1:T(8,128)(2,1)S(1)} %copy.77), channel_id=1, source_target_pairs={{0,4},{4,8},{8,12},{12,16},{16,20},{20,24},{24,28},{28,0},{1,5},{5... | collective-permute-start | bytes 49160 | tf_op jit(solution)/shard_map/while/body/eval_jaxpr/ppermute | solution.py:9
  41.1 5.6 %collective-permute-start.1 = (bf16[8,8,128]{2,0,1:T(8,128)(2,1)S(1)}, bf16[8,8,128]{2,0,1:T(8,128)(2,1)S(1)}, u32[]{:S(2)}, u32[]{:S(2)}) collective-permute-start(bf16[8,8,128]{2,0,1:T(8,128)(2,1)S(1)} %copy.78), channel_id=1, source_target_pairs={{0,4},{4,8},{8,12},{12,16},{16,20},{20,24},{24,28},{28,0},{1,5},{5... | collective-permute-start | bytes 49160 | tf_op jit(solution)/shard_map/while/body/eval_jaxpr/ppermute | solution.py:9
  42.7 3.9 %collective-permute-start.2 = (f32[8,8]{1,0:T(8,128)S(1)}, f32[8,8]{1,0:T(8,128)S(1)}, u32[]{:S(2)}, u32[]{:S(2)}) collective-permute-start(f32[8,8]{1,0:T(8,128)S(1)} %copy.79), channel_id=1, source_target_pairs={{0,4},{4,8},{8,12},{12,16},{16,20},{20,24},{24,28},{28,0},{1,5},{5... | collective-permute-start | bytes 776 | tf_op jit(solution)/shard_map/while/body/eval_jaxpr/ppermute | solution.py:9
  42.8 3.9 %collective-permute-start.3 = (f32[8,8]{1,0:T(8,128)S(1)}, f32[8,8]{1,0:T(8,128)S(1)}, u32[]{:S(2)}, u32[]{:S(2)}) collective-permute-start(f32[8,8]{1,0:T(8,128)S(1)} %copy.80), channel_id=1, source_target_pairs={{0,4},{4,8},{8,12},{12,16},{16,20},{20,24},{24,28},{28,0},{1,5},{5... | collective-permute-start | bytes 776 | tf_op jit(solution)/shard_map/while/body/eval_jaxpr/ppermute | solution.py:9
  44.5 1.0 copy-start.1
  45.9 4.3 %collective-permute-start.4 = (f32[8,8,128]{2,1,0:T(8,128)S(1)}, f32[8,8,128]{2,1,0:T(8,128)S(1)}, u32[]{:S(2)}, u32[]{:S(2)}) collective-permute-start(f32[8,8,128]{2,1,0:T(8,128)S(1)} %fusion.72), channel_id=1, source_target_pairs={{0,4},{4,8},{8,12},{12,16},{16,20},{20,24},{24,28},{28,0},{1,5},{5... | collective-permute-start | bytes 98312 | tf_op jit(solution)/shard_map/while/body/eval_jaxpr/ppermute | solution.py:9
  50.2 4.7 %collective-permute-start = (bf16[8,8,128]{2,0,1:T(8,128)(2,1)S(1)}, bf16[8,8,128]{2,0,1:T(8,128)(2,1)S(1)}, u32[]{:S(2)}, u32[]{:S(2)}) collective-permute-start(bf16[8,8,128]{2,0,1:T(8,128)(2,1)S(1)} %copy.77), channel_id=1, source_target_pairs={{0,4},{4,8},{8,12},{12,16},{16,20},{20,24},{24,28},{28,0},{1,5},{5... | collective-permute-start | bytes 49160 | tf_op jit(solution)/shard_map/while/body/eval_jaxpr/ppermute | solution.py:9
  50.2 4.7 %collective-permute-start.1 = (bf16[8,8,128]{2,0,1:T(8,128)(2,1)S(1)}, bf16[8,8,128]{2,0,1:T(8,128)(2,1)S(1)}, u32[]{:S(2)}, u32[]{:S(2)}) collective-permute-start(bf16[8,8,128]{2,0,1:T(8,128)(2,1)S(1)} %copy.78), channel_id=1, source_target_pairs={{0,4},{4,8},{8,12},{12,16},{16,20},{20,24},{24,28},{28,0},{1,5},{5... | collective-permute-start | bytes 49160 | tf_op jit(solution)/shard_map/while/body/eval_jaxpr/ppermute | solution.py:9
  50.9 3.9 %collective-permute-start.2 = (f32[8,8]{1,0:T(8,128)S(1)}, f32[8,8]{1,0:T(8,128)S(1)}, u32[]{:S(2)}, u32[]{:S(2)}) collective-permute-start(f32[8,8]{1,0:T(8,128)S(1)} %copy.79), channel_id=1, source_target_pairs={{0,4},{4,8},{8,12},{12,16},{16,20},{20,24},{24,28},{28,0},{1,5},{5... | collective-permute-start | bytes 776 | tf_op jit(solution)/shard_map/while/body/eval_jaxpr/ppermute | solution.py:9
  50.9 3.9 %collective-permute-start.3 = (f32[8,8]{1,0:T(8,128)S(1)}, f32[8,8]{1,0:T(8,128)S(1)}, u32[]{:S(2)}, u32[]{:S(2)}) collective-permute-start(f32[8,8]{1,0:T(8,128)S(1)} %copy.80), channel_id=1, source_target_pairs={{0,4},{4,8},{8,12},{12,16},{16,20},{20,24},{24,28},{28,0},{1,5},{5... | collective-permute-start | bytes 776 | tf_op jit(solution)/shard_map/while/body/eval_jaxpr/ppermute | solution.py:9
  52.5 1.0 copy-start.1
  53.9 4.3 %collective-permute-start.4 = (f32[8,8,128]{2,1,0:T(8,128)S(1)}, f32[8,8,128]{2,1,0:T(8,128)S(1)}, u32[]{:S(2)}, u32[]{:S(2)}) collective-permute-start(f32[8,8,128]{2,1,0:T(8,128)S(1)} %fusion.72), channel_id=1, source_target_pairs={{0,4},{4,8},{8,12},{12,16},{16,20},{20,24},{24,28},{28,0},{1,5},{5... | collective-permute-start | bytes 98312 | tf_op jit(solution)/shard_map/while/body/eval_jaxpr/ppermute | solution.py:9
  58.2 5.6 %collective-permute-start = (bf16[8,8,128]{2,0,1:T(8,128)(2,1)S(1)}, bf16[8,8,128]{2,0,1:T(8,128)(2,1)S(1)}, u32[]{:S(2)}, u32[]{:S(2)}) collective-permute-start(bf16[8,8,128]{2,0,1:T(8,128)(2,1)S(1)} %copy.77), channel_id=1, source_target_pairs={{0,4},{4,8},{8,12},{12,16},{16,20},{20,24},{24,28},{28,0},{1,5},{5... | collective-permute-start | bytes 49160 | tf_op jit(solution)/shard_map/while/body/eval_jaxpr/ppermute | solution.py:9
  58.2 5.6 %collective-permute-start.1 = (bf16[8,8,128]{2,0,1:T(8,128)(2,1)S(1)}, bf16[8,8,128]{2,0,1:T(8,128)(2,1)S(1)}, u32[]{:S(2)}, u32[]{:S(2)}) collective-permute-start(bf16[8,8,128]{2,0,1:T(8,128)(2,1)S(1)} %copy.78), channel_id=1, source_target_pairs={{0,4},{4,8},{8,12},{12,16},{16,20},{20,24},{24,28},{28,0},{1,5},{5... | collective-permute-start | bytes 49160 | tf_op jit(solution)/shard_map/while/body/eval_jaxpr/ppermute | solution.py:9
  58.3 5.4 %collective-permute-start.2 = (f32[8,8]{1,0:T(8,128)S(1)}, f32[8,8]{1,0:T(8,128)S(1)}, u32[]{:S(2)}, u32[]{:S(2)}) collective-permute-start(f32[8,8]{1,0:T(8,128)S(1)} %copy.79), channel_id=1, source_target_pairs={{0,4},{4,8},{8,12},{12,16},{16,20},{20,24},{24,28},{28,0},{1,5},{5... | collective-permute-start | bytes 776 | tf_op jit(solution)/shard_map/while/body/eval_jaxpr/ppermute | solution.py:9
  58.3 5.4 %collective-permute-start.3 = (f32[8,8]{1,0:T(8,128)S(1)}, f32[8,8]{1,0:T(8,128)S(1)}, u32[]{:S(2)}, u32[]{:S(2)}) collective-permute-start(f32[8,8]{1,0:T(8,128)S(1)} %copy.80), channel_id=1, source_target_pairs={{0,4},{4,8},{8,12},{12,16},{16,20},{20,24},{24,28},{28,0},{1,5},{5... | collective-permute-start | bytes 776 | tf_op jit(solution)/shard_map/while/body/eval_jaxpr/ppermute | solution.py:9
  61.6 1.0 copy-start.1
  62.9 4.3 %collective-permute-start.4 = (f32[8,8,128]{2,1,0:T(8,128)S(1)}, f32[8,8,128]{2,1,0:T(8,128)S(1)}, u32[]{:S(2)}, u32[]{:S(2)}) collective-permute-start(f32[8,8,128]{2,1,0:T(8,128)S(1)} %fusion.72), channel_id=1, source_target_pairs={{0,4},{4,8},{8,12},{12,16},{16,20},{20,24},{24,28},{28,0},{1,5},{5... | collective-permute-start | bytes 98312 | tf_op jit(solution)/shard_map/while/body/eval_jaxpr/ppermute | solution.py:9
  67.2 4.5 %collective-permute-start = (bf16[8,8,128]{2,0,1:T(8,128)(2,1)S(1)}, bf16[8,8,128]{2,0,1:T(8,128)(2,1)S(1)}, u32[]{:S(2)}, u32[]{:S(2)}) collective-permute-start(bf16[8,8,128]{2,0,1:T(8,128)(2,1)S(1)} %copy.77), channel_id=1, source_target_pairs={{0,4},{4,8},{8,12},{12,16},{16,20},{20,24},{24,28},{28,0},{1,5},{5... | collective-permute-start | bytes 49160 | tf_op jit(solution)/shard_map/while/body/eval_jaxpr/ppermute | solution.py:9
  67.2 4.5 %collective-permute-start.1 = (bf16[8,8,128]{2,0,1:T(8,128)(2,1)S(1)}, bf16[8,8,128]{2,0,1:T(8,128)(2,1)S(1)}, u32[]{:S(2)}, u32[]{:S(2)}) collective-permute-start(bf16[8,8,128]{2,0,1:T(8,128)(2,1)S(1)} %copy.78), channel_id=1, source_target_pairs={{0,4},{4,8},{8,12},{12,16},{16,20},{20,24},{24,28},{28,0},{1,5},{5... | collective-permute-start | bytes 49160 | tf_op jit(solution)/shard_map/while/body/eval_jaxpr/ppermute | solution.py:9
  67.3 4.4 %collective-permute-start.2 = (f32[8,8]{1,0:T(8,128)S(1)}, f32[8,8]{1,0:T(8,128)S(1)}, u32[]{:S(2)}, u32[]{:S(2)}) collective-permute-start(f32[8,8]{1,0:T(8,128)S(1)} %copy.79), channel_id=1, source_target_pairs={{0,4},{4,8},{8,12},{12,16},{16,20},{20,24},{24,28},{28,0},{1,5},{5... | collective-permute-start | bytes 776 | tf_op jit(solution)/shard_map/while/body/eval_jaxpr/ppermute | solution.py:9
  67.4 4.4 %collective-permute-start.3 = (f32[8,8]{1,0:T(8,128)S(1)}, f32[8,8]{1,0:T(8,128)S(1)}, u32[]{:S(2)}, u32[]{:S(2)}) collective-permute-start(f32[8,8]{1,0:T(8,128)S(1)} %copy.80), channel_id=1, source_target_pairs={{0,4},{4,8},{8,12},{12,16},{16,20},{20,24},{24,28},{28,0},{1,5},{5... | collective-permute-start | bytes 776 | tf_op jit(solution)/shard_map/while/body/eval_jaxpr/ppermute | solution.py:9
  69.6 1.0 copy-start.1
  70.9 4.3 %collective-permute-start.4 = (f32[8,8,128]{2,1,0:T(8,128)S(1)}, f32[8,8,128]{2,1,0:T(8,128)S(1)}, u32[]{:S(2)}, u32[]{:S(2)}) collective-permute-start(f32[8,8,128]{2,1,0:T(8,128)S(1)} %fusion.72), channel_id=1, source_target_pairs={{0,4},{4,8},{8,12},{12,16},{16,20},{20,24},{24,28},{28,0},{1,5},{5... | collective-permute-start | bytes 98312 | tf_op jit(solution)/shard_map/while/body/eval_jaxpr/ppermute | solution.py:9
  75.2 5.6 %collective-permute-start = (bf16[8,8,128]{2,0,1:T(8,128)(2,1)S(1)}, bf16[8,8,128]{2,0,1:T(8,128)(2,1)S(1)}, u32[]{:S(2)}, u32[]{:S(2)}) collective-permute-start(bf16[8,8,128]{2,0,1:T(8,128)(2,1)S(1)} %copy.77), channel_id=1, source_target_pairs={{0,4},{4,8},{8,12},{12,16},{16,20},{20,24},{24,28},{28,0},{1,5},{5... | collective-permute-start | bytes 49160 | tf_op jit(solution)/shard_map/while/body/eval_jaxpr/ppermute | solution.py:9
  75.2 5.6 %collective-permute-start.1 = (bf16[8,8,128]{2,0,1:T(8,128)(2,1)S(1)}, bf16[8,8,128]{2,0,1:T(8,128)(2,1)S(1)}, u32[]{:S(2)}, u32[]{:S(2)}) collective-permute-start(bf16[8,8,128]{2,0,1:T(8,128)(2,1)S(1)} %copy.78), channel_id=1, source_target_pairs={{0,4},{4,8},{8,12},{12,16},{16,20},{20,24},{24,28},{28,0},{1,5},{5... | collective-permute-start | bytes 49160 | tf_op jit(solution)/shard_map/while/body/eval_jaxpr/ppermute | solution.py:9
  75.3 5.4 %collective-permute-start.2 = (f32[8,8]{1,0:T(8,128)S(1)}, f32[8,8]{1,0:T(8,128)S(1)}, u32[]{:S(2)}, u32[]{:S(2)}) collective-permute-start(f32[8,8]{1,0:T(8,128)S(1)} %copy.79), channel_id=1, source_target_pairs={{0,4},{4,8},{8,12},{12,16},{16,20},{20,24},{24,28},{28,0},{1,5},{5... | collective-permute-start | bytes 776 | tf_op jit(solution)/shard_map/while/body/eval_jaxpr/ppermute | solution.py:9
  75.4 5.4 %collective-permute-start.3 = (f32[8,8]{1,0:T(8,128)S(1)}, f32[8,8]{1,0:T(8,128)S(1)}, u32[]{:S(2)}, u32[]{:S(2)}) collective-permute-start(f32[8,8]{1,0:T(8,128)S(1)} %copy.80), channel_id=1, source_target_pairs={{0,4},{4,8},{8,12},{12,16},{16,20},{20,24},{24,28},{28,0},{1,5},{5... | collective-permute-start | bytes 776 | tf_op jit(solution)/shard_map/while/body/eval_jaxpr/ppermute | solution.py:9
  78.6 1.0 copy-start.1
  79.9 4.3 %collective-permute-start.4 = (f32[8,8,128]{2,1,0:T(8,128)S(1)}, f32[8,8,128]{2,1,0:T(8,128)S(1)}, u32[]{:S(2)}, u32[]{:S(2)}) collective-permute-start(f32[8,8,128]{2,1,0:T(8,128)S(1)} %fusion.72), channel_id=1, source_target_pairs={{0,4},{4,8},{8,12},{12,16},{16,20},{20,24},{24,28},{28,0},{1,5},{5... | collective-permute-start | bytes 98312 | tf_op jit(solution)/shard_map/while/body/eval_jaxpr/ppermute | solution.py:9
  84.2 4.5 %collective-permute-start = (bf16[8,8,128]{2,0,1:T(8,128)(2,1)S(1)}, bf16[8,8,128]{2,0,1:T(8,128)(2,1)S(1)}, u32[]{:S(2)}, u32[]{:S(2)}) collective-permute-start(bf16[8,8,128]{2,0,1:T(8,128)(2,1)S(1)} %copy.77), channel_id=1, source_target_pairs={{0,4},{4,8},{8,12},{12,16},{16,20},{20,24},{24,28},{28,0},{1,5},{5... | collective-permute-start | bytes 49160 | tf_op jit(solution)/shard_map/while/body/eval_jaxpr/ppermute | solution.py:9
  84.2 4.5 %collective-permute-start.1 = (bf16[8,8,128]{2,0,1:T(8,128)(2,1)S(1)}, bf16[8,8,128]{2,0,1:T(8,128)(2,1)S(1)}, u32[]{:S(2)}, u32[]{:S(2)}) collective-permute-start(bf16[8,8,128]{2,0,1:T(8,128)(2,1)S(1)} %copy.78), channel_id=1, source_target_pairs={{0,4},{4,8},{8,12},{12,16},{16,20},{20,24},{24,28},{28,0},{1,5},{5... | collective-permute-start | bytes 49160 | tf_op jit(solution)/shard_map/while/body/eval_jaxpr/ppermute | solution.py:9
  84.3 4.4 %collective-permute-start.2 = (f32[8,8]{1,0:T(8,128)S(1)}, f32[8,8]{1,0:T(8,128)S(1)}, u32[]{:S(2)}, u32[]{:S(2)}) collective-permute-start(f32[8,8]{1,0:T(8,128)S(1)} %copy.79), channel_id=1, source_target_pairs={{0,4},{4,8},{8,12},{12,16},{16,20},{20,24},{24,28},{28,0},{1,5},{5... | collective-permute-start | bytes 776 | tf_op jit(solution)/shard_map/while/body/eval_jaxpr/ppermute | solution.py:9
  84.4 4.4 %collective-permute-start.3 = (f32[8,8]{1,0:T(8,128)S(1)}, f32[8,8]{1,0:T(8,128)S(1)}, u32[]{:S(2)}, u32[]{:S(2)}) collective-permute-start(f32[8,8]{1,0:T(8,128)S(1)} %copy.80), channel_id=1, source_target_pairs={{0,4},{4,8},{8,12},{12,16},{16,20},{20,24},{24,28},{28,0},{1,5},{5... | collective-permute-start | bytes 776 | tf_op jit(solution)/shard_map/while/body/eval_jaxpr/ppermute | solution.py:9
  88.0 4.3 %collective-permute-start.4 = (f32[8,8,128]{2,1,0:T(8,128)S(1)}, f32[8,8,128]{2,1,0:T(8,128)S(1)}, u32[]{:S(2)}, u32[]{:S(2)}) collective-permute-start(f32[8,8,128]{2,1,0:T(8,128)S(1)} %fusion.72), channel_id=1, source_target_pairs={{0,4},{4,8},{8,12},{12,16},{16,20},{20,24},{24,28},{28,0},{1,5},{5... | collective-permute-start | bytes 98312 | tf_op jit(solution)/shard_map/while/body/eval_jaxpr/ppermute | solution.py:9
  92.3 5.6 %collective-permute-start = (bf16[8,8,128]{2,0,1:T(8,128)(2,1)S(1)}, bf16[8,8,128]{2,0,1:T(8,128)(2,1)S(1)}, u32[]{:S(2)}, u32[]{:S(2)}) collective-permute-start(bf16[8,8,128]{2,0,1:T(8,128)(2,1)S(1)} %copy.77), channel_id=1, source_target_pairs={{0,4},{4,8},{8,12},{12,16},{16,20},{20,24},{24,28},{28,0},{1,5},{5... | collective-permute-start | bytes 49160 | tf_op jit(solution)/shard_map/while/body/eval_jaxpr/ppermute | solution.py:9
  92.3 5.6 %collective-permute-start.1 = (bf16[8,8,128]{2,0,1:T(8,128)(2,1)S(1)}, bf16[8,8,128]{2,0,1:T(8,128)(2,1)S(1)}, u32[]{:S(2)}, u32[]{:S(2)}) collective-permute-start(bf16[8,8,128]{2,0,1:T(8,128)(2,1)S(1)} %copy.78), channel_id=1, source_target_pairs={{0,4},{4,8},{8,12},{12,16},{16,20},{20,24},{24,28},{28,0},{1,5},{5... | collective-permute-start | bytes 49160 | tf_op jit(solution)/shard_map/while/body/eval_jaxpr/ppermute | solution.py:9
  92.3 5.5 %collective-permute-start.2 = (f32[8,8]{1,0:T(8,128)S(1)}, f32[8,8]{1,0:T(8,128)S(1)}, u32[]{:S(2)}, u32[]{:S(2)}) collective-permute-start(f32[8,8]{1,0:T(8,128)S(1)} %copy.79), channel_id=1, source_target_pairs={{0,4},{4,8},{8,12},{12,16},{16,20},{20,24},{24,28},{28,0},{1,5},{5... | collective-permute-start | bytes 776 | tf_op jit(solution)/shard_map/while/body/eval_jaxpr/ppermute | solution.py:9
  92.4 5.4 %collective-permute-start.3 = (f32[8,8]{1,0:T(8,128)S(1)}, f32[8,8]{1,0:T(8,128)S(1)}, u32[]{:S(2)}, u32[]{:S(2)}) collective-permute-start(f32[8,8]{1,0:T(8,128)S(1)} %copy.80), channel_id=1, source_target_pairs={{0,4},{4,8},{8,12},{12,16},{16,20},{20,24},{24,28},{28,0},{1,5},{5... | collective-permute-start | bytes 776 | tf_op jit(solution)/shard_map/while/body/eval_jaxpr/ppermute | solution.py:9
  97.0 4.3 %collective-permute-start.4 = (f32[8,8,128]{2,1,0:T(8,128)S(1)}, f32[8,8,128]{2,1,0:T(8,128)S(1)}, u32[]{:S(2)}, u32[]{:S(2)}) collective-permute-start(f32[8,8,128]{2,1,0:T(8,128)S(1)} %fusion.72), channel_id=1, source_target_pairs={{0,4},{4,8},{8,12},{12,16},{16,20},{20,24},{24,28},{28,0},{1,5},{5... | collective-permute-start | bytes 98312 | tf_op jit(solution)/shard_map/while/body/eval_jaxpr/ppermute | solution.py:9
  102.6 4.2 %collective-permute-start.5 = (bf16[8,8,128]{2,1,0:T(8,128)(2,1)S(1)}, bf16[8,8,128]{2,1,0:T(8,128)(2,1)}, u32[]{:S(2)}, u32[]{:S(2)}) collective-permute-start(bf16[8,8,128]{2,1,0:T(8,128)(2,1)S(1)} %fusion.32), channel_id=1, source_target_pairs={{0,4},{4,8},{8,12},{12,16},{16,20},{20,24},{24,28},{28,0},{1,5},{5... | collective-permute-start | bytes 49160 | tf_op jit(solution)/shard_map/ppermute | solution.py:9
  106.9 8.8 %all-to-all-start.4 = ((bf16[8,8,128]{2,1,0:T(8,128)(2,1)}), bf16[8,8,128]{2,1,0:T(8,128)(2,1)S(1)}, u32[]{:S(2)}, u32[]{:S(2)}) async-start(bf16[8,8,128]{2,1,0:T(8,128)(2,1)} %collective-permute-done.5), calls=%async_computation.4 | async-start | bytes 32768 | tf_op jit(solution)/shard_map/all_to_all | solution.py:99
  (4 other events, 3.5 us)
where the time goes:
time: 117 us; the launch traced here: 116 us
  waiting for transfers between devices  50 us (43%)
  starting transfers between devices  39.4 us (34%)
  local copies, waits for them, and re-layouts  12.4 us (11%)
  matrix products  11.5 us (10%)
  other arithmetic  1.51 us (1%)
    ppermute x36, waiting for transfers between devices, shifted(): lax.ppermute(value, axis, [(i, (i + by) % peers) for i in range(peers)])  27.5 us
    ppermute x36, starting transfers between devices, shifted(): lax.ppermute(value, axis, [(i, (i + by) % peers) for i in range(peers)])  20.1 us
    all_to_all x1, starting transfers between devices, local(): lax.all_to_all(log_norms, 'kvh', split_axis=1, concat_axis=0, tiled=True)  6.35 us
    all_to_all x1, waiting for transfers between devices, local(): lax.all_to_all(deltas, 'kvh', split_axis=1, concat_axis=0, tiled=True)  5.48 us
    while x42, local copies, waits for them, and re-layouts  5.07 us
    all_to_all x1, waiting for transfers between devices, local(): lax.all_to_all(query_grad.astype(jnp.bfloat16), 'kvh', split_axis=0, conc...  4.59 us
    all_to_all x1, waiting for transfers between devices, local(): lax.all_to_all(log_norms, 'kvh', split_axis=1, concat_axis=0, tiled=True)  4.21 us
    all_to_all x1, waiting for transfers between devices, local(): lax.all_to_all(queries, 'kvh', split_axis=1, concat_axis=0, tiled=True)  4.16 us
  transfers between devices with their start and end apart: 41, of which 16 were waited for; matrix products, arithmetic and copies ran while one was open for 14% of the time, Pallas kernels for 0%

commit v1 on v0

--- a/solution.py
+++ b/solution.py
@@ -15,7 +15,12 @@
     seq_index = lax.axis_index("seq")
     deltas = jnp.sum(grad_out.astype(jnp.float32) * attn_out.astype(jnp.float32), axis=-1)
     query_block, grad_block = (
-        lax.all_to_all(queries, "kvh", split_axis=1, concat_axis=0, tiled=True),
+        jnp.concatenate(
+            lax.all_to_all(
+                jnp.stack(jnp.split(queries, lax.axis_size("kvh"), axis=1)), "kvh", 0, 0
+            ),
+            axis=0,
+        ),
         lax.all_to_all(grad_out, "kvh", split_axis=1, concat_axis=0, tiled=True),
     )
     norm_block, delta_block = (

time: 117 us -> 117 us (level)
  local copies, waits for them, and re-layouts: 12.4 us -> 11.1 us
    unnamed x10 -> x9, local copies, waits for them, and re-layouts: 3.33 us -> 2.72 us
  transfers between devices with their start and end apart: 41 -> 41, of which waited for: 16 -> 16; matrix products, arithmetic and copies ran while one was open for 14% -> 13% of each run, Pallas kernels for 0% -> 0%
where the time goes in v1:
time: 117 us; the launch traced here: 116 us
  waiting for transfers between devices  50 us (43%)
  starting transfers between devices  39.5 us (34%)
  matrix products  11.5 us (10%)
  local copies, waits for them, and re-layouts  11.1 us (9%)
  other arithmetic  2.13 us (2%)
    ppermute x36, waiting for transfers between devices, shifted(): lax.ppermute(value, axis, [(i, (i + by) % peers) for i in range(peers)])  27.5 us
    ppermute x36, starting transfers between devices, shifted(): lax.ppermute(value, axis, [(i, (i + by) % peers) for i in range(peers)])  20.2 us
    all_to_all x1, starting transfers between devices, local(): lax.all_to_all(log_norms, 'kvh', split_axis=1, concat_axis=0, tiled=True)  6.35 us
    all_to_all x1, waiting for transfers between devices, local(): lax.all_to_all(deltas, 'kvh', split_axis=1, concat_axis=0, tiled=True)  5.41 us
    while x42, local copies, waits for them, and re-layouts  5.08 us
    all_to_all x1, waiting for transfers between devices, local(): lax.all_to_all(query_grad.astype(jnp.bfloat16), 'kvh', split_axis=0, conc...  4.59 us
    all_to_all x1, waiting for transfers between devices, local(): lax.all_to_all(jnp.stack(jnp.split(queries, lax.axis_size('kvh'), axis=1)...  4.23 us
    all_to_all x1, waiting for transfers between devices, local(): lax.all_to_all(grad_out, 'kvh', split_axis=1, concat_axis=0, tiled=True)  4.15 us
  transfers between devices with their start and end apart: 41, of which 16 were waited for; matrix products, arithmetic and copies ran while one was open for 13% of the time, Pallas kernels for 0%

profile of v1, /device:TPU:0, one launch (start us, length us, event | category | flops | bytes accessed | tf_op | source)
XLA Modules:
  0.0 115.7 jit_solution(5973198369871653567)
XLA Ops:
  0.7 0.8 all_to_all.62
  1.5 0.6 copy.30
  2.1 6.3 %all-to-all-start.2 = ((f32[2,4,8]{2,0,1:T(2,128)}), f32[2,4,8]{2,0,1:T(2,128)S(1)}, u32[]{:S(2)}, u32[]{:S(2)}) async-start(f32[2,4,8]{2,0,1:T(2,128)} %copy.30), calls=%async_computation.2 | async-start | bytes 8192 | tf_op jit(solution)/shard_map/all_to_all | solution.py:27
  8.4 0.8 multiply_reduce_fusion
  9.2 0.6 pad_maximum_fusion
  9.8 4.1 %all-to-all-done.2 = f32[2,4,8]{2,0,1:T(2,128)S(1)} async-done(((f32[2,4,8]{2,0,1:T(2,128)}), f32[2,4,8]{2,0,1:T(2,128)S(1)}, u32[]{:S(2)}, u32[]{:S(2)}) %all-to-all-start.2) | async-done | bytes 288 | tf_op jit(solution)/shard_map/all_to_all | solution.py:27
  14.0 3.3 %all-to-all-start = ((bf16[4,2,8,128]{3,2,1,0:T(8,128)(2,1)}), bf16[4,2,8,128]{3,2,1,0:T(8,128)(2,1)S(1)}, u32[]{:S(2)}, u32[]{:S(2)}) async-start(bf16[4,2,8,128]{3,2,1,0:T(8,128)(2,1)} %pad_maximum_fusion), calls=%async_computation | async-start | bytes 32768 | tf_op jit(solution)/shard_map/all_to_all | solution.py:19
  17.3 1.3 %copy.28 = bf16[2,32,128]{2,0,1:T(2,128)(2,1)} copy(bf16[2,32,128]{2,1,0:T(8,128)(2,1)} %param.11) | data formatting | bytes 32768 | tf_op args[2]
  18.6 4.2 %all-to-all-done = bf16[4,2,8,128]{3,2,1,0:T(8,128)(2,1)S(1)} async-done(((bf16[4,2,8,128]{3,2,1,0:T(8,128)(2,1)}), bf16[4,2,8,128]{3,2,1,0:T(8,128)(2,1)S(1)}, u32[]{:S(2)}, u32[]{:S(2)}) %all-to-all-start) | async-done | bytes 16416 | tf_op jit(solution)/shard_map/all_to_all | solution.py:19
  22.8 3.3 %all-to-all-start.1 = ((bf16[2,32,128]{2,0,1:T(2,128)(2,1)}), bf16[2,32,128]{2,0,1:T(2,128)(2,1)S(1)}, u32[]{:S(2)}, u32[]{:S(2)}) async-start(bf16[2,32,128]{2,0,1:T(2,128)(2,1)} %copy.28), calls=%async_computation.1 | async-start | bytes 32768 | tf_op jit(solution)/shard_map/all_to_all | solution.py:24
  26.2 0.6 copy.31
  26.8 0.7 copy-done.4
  27.5 4.1 %all-to-all-done.1 = bf16[2,32,128]{2,0,1:T(2,128)(2,1)S(1)} async-done(((bf16[2,32,128]{2,0,1:T(2,128)(2,1)}), bf16[2,32,128]{2,0,1:T(2,128)(2,1)S(1)}, u32[]{:S(2)}, u32[]{:S(2)}) %all-to-all-start.1) | async-done | bytes 16416 | tf_op jit(solution)/shard_map/all_to_all | solution.py:24
  31.7 3.2 %all-to-all-start.3 = ((f32[2,4,8]{2,0,1:T(2,128)}), f32[2,4,8]{2,0,1:T(2,128)S(1)}, u32[]{:S(2)}, u32[]{:S(2)}) async-start(f32[2,4,8]{2,0,1:T(2,128)} %copy.31), calls=%async_computation.3 | async-start | bytes 8192 | tf_op jit(solution)/shard_map/all_to_all | solution.py:28
  35.1 5.4 %all-to-all-done.3 = f32[2,4,8]{2,0,1:T(2,128)S(1)} async-done(((f32[2,4,8]{2,0,1:T(2,128)}), f32[2,4,8]{2,0,1:T(2,128)S(1)}, u32[]{:S(2)}, u32[]{:S(2)}) %all-to-all-start.3) | async-done | bytes 288 | tf_op jit(solution)/shard_map/all_to_all | solution.py:28
  40.5 60.2 %while.28 = (s32[]{:T(128)}, bf16[8,8,128]{2,0,1:T(8,128)(2,1)S(1)}, bf16[8,8,128]{2,0,1:T(8,128)(2,1)S(1)}, f32[8,8]{1,0:T(8,128)S(1)}, f32[8,8]{1,0:T(8,128)S(...) while((s32[]{:T(128)}, ...), condition=%wide.region_2.3_spmd.clone, body=%wide.region_1.2_spmd.clone.sunk | while | flops 85042200 | bytes 5599483 | solution.py:93
  40.6 1.6 %collective-permute-start.1 = (bf16[8,8,128]{2,0,1:T(8,128)(2,1)S(1)}, bf16[8,8,128]{2,0,1:T(8,128)(2,1)S(1)}, u32[]{:S(2)}, u32[]{:S(2)}) collective-permute-start(bf16[8,8,128]{2,0,1:T(8,128)(2,1)S(1)} %copy.77), channel_id=1, source_target_pairs={{0,4},{4,8},{8,12},{12,16},{16,20},{20,24},{24,28},{28,0},{1,5},{5... | collective-permute-start | bytes 49160 | tf_op jit(solution)/shard_map/while/body/eval_jaxpr/ppermute | solution.py:9
  42.2 1.5 %collective-permute-start.3 = (f32[8,8]{1,0:T(8,128)S(1)}, f32[8,8]{1,0:T(8,128)S(1)}, u32[]{:S(2)}, u32[]{:S(2)}) collective-permute-start(f32[8,8]{1,0:T(8,128)S(1)} %copy.79), channel_id=1, source_target_pairs={{0,4},{4,8},{8,12},{12,16},{16,20},{20,24},{24,28},{28,0},{1,5},{5... | collective-permute-start | bytes 776 | tf_op jit(solution)/shard_map/while/body/eval_jaxpr/ppermute | solution.py:9
  44.1 0.7 copy-done.1
  46.2 3.4 %collective-permute-done.4 = f32[8,8,128]{2,1,0:T(8,128)S(1)} collective-permute-done((f32[8,8,128]{2,1,0:T(8,128)S(1)}, f32[8,8,128]{2,1,0:T(8,128)S(1)}, u32[]{:S(2)}, u32[]{:S(2)}) %collective-permute-start.4) | collective-permute-done | bytes 32800 | tf_op jit(solution)/shard_map/while/body/eval_jaxpr/ppermute | solution.py:9
  49.6 0.7 collective-permute-start.1
  50.3 1.4 %collective-permute-start.3 = (f32[8,8]{1,0:T(8,128)S(1)}, f32[8,8]{1,0:T(8,128)S(1)}, u32[]{:S(2)}, u32[]{:S(2)}) collective-permute-start(f32[8,8]{1,0:T(8,128)S(1)} %copy.79), channel_id=1, source_target_pairs={{0,4},{4,8},{8,12},{12,16},{16,20},{20,24},{24,28},{28,0},{1,5},{5... | collective-permute-start | bytes 776 | tf_op jit(solution)/shard_map/while/body/eval_jaxpr/ppermute | solution.py:9
  52.2 0.7 copy-done.1
  53.7 0.3 fusion.73
  54.3 3.3 %collective-permute-done.4 = f32[8,8,128]{2,1,0:T(8,128)S(1)} collective-permute-done((f32[8,8,128]{2,1,0:T(8,128)S(1)}, f32[8,8,128]{2,1,0:T(8,128)S(1)}, u32[]{:S(2)}, u32[]{:S(2)}) %collective-permute-start.4) | collective-permute-done | bytes 32800 | tf_op jit(solution)/shard_map/while/body/eval_jaxpr/ppermute | solution.py:9
  57.7 3.1 %collective-permute-start.3 = (f32[8,8]{1,0:T(8,128)S(1)}, f32[8,8]{1,0:T(8,128)S(1)}, u32[]{:S(2)}, u32[]{:S(2)}) collective-permute-start(f32[8,8]{1,0:T(8,128)S(1)} %copy.79), channel_id=1, source_target_pairs={{0,4},{4,8},{8,12},{12,16},{16,20},{20,24},{24,28},{28,0},{1,5},{5... | collective-permute-start | bytes 776 | tf_op jit(solution)/shard_map/while/body/eval_jaxpr/ppermute | solution.py:9
  61.2 0.7 copy-done.1
  62.8 0.3 fusion.73
  63.1 3.5 %collective-permute-done.4 = f32[8,8,128]{2,1,0:T(8,128)S(1)} collective-permute-done((f32[8,8,128]{2,1,0:T(8,128)S(1)}, f32[8,8,128]{2,1,0:T(8,128)S(1)}, u32[]{:S(2)}, u32[]{:S(2)}) %collective-permute-start.4) | collective-permute-done | bytes 32800 | tf_op jit(solution)/shard_map/while/body/eval_jaxpr/ppermute | solution.py:9
  66.8 2.0 %collective-permute-start.3 = (f32[8,8]{1,0:T(8,128)S(1)}, f32[8,8]{1,0:T(8,128)S(1)}, u32[]{:S(2)}, u32[]{:S(2)}) collective-permute-start(f32[8,8]{1,0:T(8,128)S(1)} %copy.79), channel_id=1, source_target_pairs={{0,4},{4,8},{8,12},{12,16},{16,20},{20,24},{24,28},{28,0},{1,5},{5... | collective-permute-start | bytes 776 | tf_op jit(solution)/shard_map/while/body/eval_jaxpr/ppermute | solution.py:9
  69.2 0.7 copy-done.1
  71.2 3.5 %collective-permute-done.4 = f32[8,8,128]{2,1,0:T(8,128)S(1)} collective-permute-done((f32[8,8,128]{2,1,0:T(8,128)S(1)}, f32[8,8,128]{2,1,0:T(8,128)S(1)}, u32[]{:S(2)}, u32[]{:S(2)}) %collective-permute-start.4) | collective-permute-done | bytes 32800 | tf_op jit(solution)/shard_map/while/body/eval_jaxpr/ppermute | solution.py:9
  74.8 3.1 %collective-permute-start.3 = (f32[8,8]{1,0:T(8,128)S(1)}, f32[8,8]{1,0:T(8,128)S(1)}, u32[]{:S(2)}, u32[]{:S(2)}) collective-permute-start(f32[8,8]{1,0:T(8,128)S(1)} %copy.79), channel_id=1, source_target_pairs={{0,4},{4,8},{8,12},{12,16},{16,20},{20,24},{24,28},{28,0},{1,5},{5... | collective-permute-start | bytes 776 | tf_op jit(solution)/shard_map/while/body/eval_jaxpr/ppermute | solution.py:9
  78.2 0.7 copy-done.1
  80.2 3.5 %collective-permute-done.4 = f32[8,8,128]{2,1,0:T(8,128)S(1)} collective-permute-done((f32[8,8,128]{2,1,0:T(8,128)S(1)}, f32[8,8,128]{2,1,0:T(8,128)S(1)}, u32[]{:S(2)}, u32[]{:S(2)}) %collective-permute-start.4) | collective-permute-done | bytes 32800 | tf_op jit(solution)/shard_map/while/body/eval_jaxpr/ppermute | solution.py:9
  83.8 2.0 %collective-permute-start.3 = (f32[8,8]{1,0:T(8,128)S(1)}, f32[8,8]{1,0:T(8,128)S(1)}, u32[]{:S(2)}, u32[]{:S(2)}) collective-permute-start(f32[8,8]{1,0:T(8,128)S(1)} %copy.79), channel_id=1, source_target_pairs={{0,4},{4,8},{8,12},{12,16},{16,20},{20,24},{24,28},{28,0},{1,5},{5... | collective-permute-start | bytes 776 | tf_op jit(solution)/shard_map/while/body/eval_jaxpr/ppermute | solution.py:9
  86.3 0.7 copy-done.1
  88.2 3.5 %collective-permute-done.4 = f32[8,8,128]{2,1,0:T(8,128)S(1)} collective-permute-done((f32[8,8,128]{2,1,0:T(8,128)S(1)}, f32[8,8,128]{2,1,0:T(8,128)S(1)}, u32[]{:S(2)}, u32[]{:S(2)}) %collective-permute-start.4) | collective-permute-done | bytes 32800 | tf_op jit(solution)/shard_map/while/body/eval_jaxpr/ppermute | solution.py:9
  91.8 3.1 %collective-permute-start.3 = (f32[8,8]{1,0:T(8,128)S(1)}, f32[8,8]{1,0:T(8,128)S(1)}, u32[]{:S(2)}, u32[]{:S(2)}) collective-permute-start(f32[8,8]{1,0:T(8,128)S(1)} %copy.79), channel_id=1, source_target_pairs={{0,4},{4,8},{8,12},{12,16},{16,20},{20,24},{24,28},{28,0},{1,5},{5... | collective-permute-start | bytes 776 | tf_op jit(solution)/shard_map/while/body/eval_jaxpr/ppermute | solution.py:9
  95.3 0.7 copy-done.1
  97.2 3.5 %collective-permute-done.4 = f32[8,8,128]{2,1,0:T(8,128)S(1)} collective-permute-done((f32[8,8,128]{2,1,0:T(8,128)S(1)}, f32[8,8,128]{2,1,0:T(8,128)S(1)}, u32[]{:S(2)}, u32[]{:S(2)}) %collective-permute-start.4) | collective-permute-done | bytes 32800 | tf_op jit(solution)/shard_map/while/body/eval_jaxpr/ppermute | solution.py:9
  100.9 0.7 copy-done.2
  102.1 1.0 fusion.24
  103.1 3.2 %collective-permute-done.5 = bf16[8,8,128]{2,1,0:T(8,128)(2,1)} collective-permute-done((bf16[8,8,128]{2,1,0:T(8,128)(2,1)S(1)}, bf16[8,8,128]{2,1,0:T(8,128)(2,1)}, u32[]{:S(2)}, u32[]{:S(2)}) %collective-permute-start.5) | collective-permute-done | bytes 16416 | tf_op jit(solution)/shard_map/ppermute | solution.py:9
  106.3 3.2 %all-to-all-start.4 = ((bf16[8,8,128]{2,1,0:T(8,128)(2,1)}), bf16[8,8,128]{2,1,0:T(8,128)(2,1)S(1)}, u32[]{:S(2)}, u32[]{:S(2)}) async-start(bf16[8,8,128]{2,1,0:T(8,128)(2,1)} %collective-permute-done.5), calls=%async_computation.4 | async-start | bytes 32768 | tf_op jit(solution)/shard_map/all_to_all | solution.py:104
  109.5 1.0 fusion.29
  110.5 4.6 %all-to-all-done.4 = bf16[8,8,128]{2,1,0:T(8,128)(2,1)S(1)} async-done(((bf16[8,8,128]{2,1,0:T(8,128)(2,1)}), bf16[8,8,128]{2,1,0:T(8,128)(2,1)S(1)}, u32[]{:S(2)}, u32[]{:S(2)}) %all-to-all-start.4) | async-done | bytes 16416 | tf_op jit(solution)/shard_map/all_to_all | solution.py:104
  115.1 0.6 copy.58
  (171 shorter events, 12.3 us)
Async XLA Ops:
  0.6 7.8 %copy-start.3 = (bf16[2,32,128]{2,1,0:T(8,128)(2,1)S(1)}, bf16[2,32,128]{2,1,0:T(8,128)(2,1)}, u32[]{:S(2)}) copy-start(bf16[2,32,128]{2,1,0:T(8,128)(2,1)} %param.9) | copy-start | bytes 49156
  0.6 39.8 %copy-start = (bf16[1024,1,128]{2,0,1:T(8,128)(2,1)S(1)}, bf16[1024,1,128]{2,0,1:T(8,128)(2,1)}, u32[]{:S(2)}) copy-start(bf16[1024,1,128]{2,0,1:T(8,128)(2,1)} %param.14) | copy-start | bytes 786436
  2.1 11.9 %all-to-all-start.2 = ((f32[2,4,8]{2,0,1:T(2,128)}), f32[2,4,8]{2,0,1:T(2,128)S(1)}, u32[]{:S(2)}, u32[]{:S(2)}) async-start(f32[2,4,8]{2,0,1:T(2,128)} %copy.30), calls=%async_computation.2 | async-start | bytes 8192 | tf_op jit(solution)/shard_map/all_to_all | solution.py:27
  14.0 8.8 %all-to-all-start = ((bf16[4,2,8,128]{3,2,1,0:T(8,128)(2,1)}), bf16[4,2,8,128]{3,2,1,0:T(8,128)(2,1)S(1)}, u32[]{:S(2)}, u32[]{:S(2)}) async-start(bf16[4,2,8,128]{3,2,1,0:T(8,128)(2,1)} %pad_maximum_fusion), calls=%async_computation | async-start | bytes 32768 | tf_op jit(solution)/shard_map/all_to_all | solution.py:19
  22.8 8.8 %all-to-all-start.1 = ((bf16[2,32,128]{2,0,1:T(2,128)(2,1)}), bf16[2,32,128]{2,0,1:T(2,128)(2,1)S(1)}, u32[]{:S(2)}, u32[]{:S(2)}) async-start(bf16[2,32,128]{2,0,1:T(2,128)(2,1)} %copy.28), calls=%async_computation.1 | async-start | bytes 32768 | tf_op jit(solution)/shard_map/all_to_all | solution.py:24
  31.7 8.8 %all-to-all-start.3 = ((f32[2,4,8]{2,0,1:T(2,128)}), f32[2,4,8]{2,0,1:T(2,128)S(1)}, u32[]{:S(2)}, u32[]{:S(2)}) async-start(f32[2,4,8]{2,0,1:T(2,128)} %copy.31), calls=%async_computation.3 | async-start | bytes 8192 | tf_op jit(solution)/shard_map/all_to_all | solution.py:28
  40.5 5.7 %collective-permute-start = (bf16[8,8,128]{2,0,1:T(8,128)(2,1)S(1)}, bf16[8,8,128]{2,0,1:T(8,128)(2,1)S(1)}, u32[]{:S(2)}, u32[]{:S(2)}) collective-permute-start(bf16[8,8,128]{2,0,1:T(8,128)(2,1)S(1)} %copy.76), channel_id=1, source_target_pairs={{0,4},{4,8},{8,12},{12,16},{16,20},{20,24},{24,28},{28,0},{1,5},{5... | collective-permute-start | bytes 49160 | tf_op jit(solution)/shard_map/while/body/eval_jaxpr/ppermute | solution.py:9
  40.6 5.6 %collective-permute-start.1 = (bf16[8,8,128]{2,0,1:T(8,128)(2,1)S(1)}, bf16[8,8,128]{2,0,1:T(8,128)(2,1)S(1)}, u32[]{:S(2)}, u32[]{:S(2)}) collective-permute-start(bf16[8,8,128]{2,0,1:T(8,128)(2,1)S(1)} %copy.77), channel_id=1, source_target_pairs={{0,4},{4,8},{8,12},{12,16},{16,20},{20,24},{24,28},{28,0},{1,5},{5... | collective-permute-start | bytes 49160 | tf_op jit(solution)/shard_map/while/body/eval_jaxpr/ppermute | solution.py:9
  42.1 3.9 %collective-permute-start.2 = (f32[8,8]{1,0:T(8,128)S(1)}, f32[8,8]{1,0:T(8,128)S(1)}, u32[]{:S(2)}, u32[]{:S(2)}) collective-permute-start(f32[8,8]{1,0:T(8,128)S(1)} %copy.78), channel_id=1, source_target_pairs={{0,4},{4,8},{8,12},{12,16},{16,20},{20,24},{24,28},{28,0},{1,5},{5... | collective-permute-start | bytes 776 | tf_op jit(solution)/shard_map/while/body/eval_jaxpr/ppermute | solution.py:9
  42.2 3.9 %collective-permute-start.3 = (f32[8,8]{1,0:T(8,128)S(1)}, f32[8,8]{1,0:T(8,128)S(1)}, u32[]{:S(2)}, u32[]{:S(2)}) collective-permute-start(f32[8,8]{1,0:T(8,128)S(1)} %copy.79), channel_id=1, source_target_pairs={{0,4},{4,8},{8,12},{12,16},{16,20},{20,24},{24,28},{28,0},{1,5},{5... | collective-permute-start | bytes 776 | tf_op jit(solution)/shard_map/while/body/eval_jaxpr/ppermute | solution.py:9
  43.9 1.0 copy-start.1
  45.3 4.3 %collective-permute-start.4 = (f32[8,8,128]{2,1,0:T(8,128)S(1)}, f32[8,8,128]{2,1,0:T(8,128)S(1)}, u32[]{:S(2)}, u32[]{:S(2)}) collective-permute-start(f32[8,8,128]{2,1,0:T(8,128)S(1)} %fusion.72), channel_id=1, source_target_pairs={{0,4},{4,8},{8,12},{12,16},{16,20},{20,24},{24,28},{28,0},{1,5},{5... | collective-permute-start | bytes 98312 | tf_op jit(solution)/shard_map/while/body/eval_jaxpr/ppermute | solution.py:9
  49.6 4.7 %collective-permute-start = (bf16[8,8,128]{2,0,1:T(8,128)(2,1)S(1)}, bf16[8,8,128]{2,0,1:T(8,128)(2,1)S(1)}, u32[]{:S(2)}, u32[]{:S(2)}) collective-permute-start(bf16[8,8,128]{2,0,1:T(8,128)(2,1)S(1)} %copy.76), channel_id=1, source_target_pairs={{0,4},{4,8},{8,12},{12,16},{16,20},{20,24},{24,28},{28,0},{1,5},{5... | collective-permute-start | bytes 49160 | tf_op jit(solution)/shard_map/while/body/eval_jaxpr/ppermute | solution.py:9
  49.6 4.7 %collective-permute-start.1 = (bf16[8,8,128]{2,0,1:T(8,128)(2,1)S(1)}, bf16[8,8,128]{2,0,1:T(8,128)(2,1)S(1)}, u32[]{:S(2)}, u32[]{:S(2)}) collective-permute-start(bf16[8,8,128]{2,0,1:T(8,128)(2,1)S(1)} %copy.77), channel_id=1, source_target_pairs={{0,4},{4,8},{8,12},{12,16},{16,20},{20,24},{24,28},{28,0},{1,5},{5... | collective-permute-start | bytes 49160 | tf_op jit(solution)/shard_map/while/body/eval_jaxpr/ppermute | solution.py:9
  50.3 3.9 %collective-permute-start.2 = (f32[8,8]{1,0:T(8,128)S(1)}, f32[8,8]{1,0:T(8,128)S(1)}, u32[]{:S(2)}, u32[]{:S(2)}) collective-permute-start(f32[8,8]{1,0:T(8,128)S(1)} %copy.78), channel_id=1, source_target_pairs={{0,4},{4,8},{8,12},{12,16},{16,20},{20,24},{24,28},{28,0},{1,5},{5... | collective-permute-start | bytes 776 | tf_op jit(solution)/shard_map/while/body/eval_jaxpr/ppermute | solution.py:9
  50.3 3.9 %collective-permute-start.3 = (f32[8,8]{1,0:T(8,128)S(1)}, f32[8,8]{1,0:T(8,128)S(1)}, u32[]{:S(2)}, u32[]{:S(2)}) collective-permute-start(f32[8,8]{1,0:T(8,128)S(1)} %copy.79), channel_id=1, source_target_pairs={{0,4},{4,8},{8,12},{12,16},{16,20},{20,24},{24,28},{28,0},{1,5},{5... | collective-permute-start | bytes 776 | tf_op jit(solution)/shard_map/while/body/eval_jaxpr/ppermute | solution.py:9
  51.9 1.0 copy-start.1
  53.3 4.3 %collective-permute-start.4 = (f32[8,8,128]{2,1,0:T(8,128)S(1)}, f32[8,8,128]{2,1,0:T(8,128)S(1)}, u32[]{:S(2)}, u32[]{:S(2)}) collective-permute-start(f32[8,8,128]{2,1,0:T(8,128)S(1)} %fusion.72), channel_id=1, source_target_pairs={{0,4},{4,8},{8,12},{12,16},{16,20},{20,24},{24,28},{28,0},{1,5},{5... | collective-permute-start | bytes 98312 | tf_op jit(solution)/shard_map/while/body/eval_jaxpr/ppermute | solution.py:9
  57.6 5.6 %collective-permute-start = (bf16[8,8,128]{2,0,1:T(8,128)(2,1)S(1)}, bf16[8,8,128]{2,0,1:T(8,128)(2,1)S(1)}, u32[]{:S(2)}, u32[]{:S(2)}) collective-permute-start(bf16[8,8,128]{2,0,1:T(8,128)(2,1)S(1)} %copy.76), channel_id=1, source_target_pairs={{0,4},{4,8},{8,12},{12,16},{16,20},{20,24},{24,28},{28,0},{1,5},{5... | collective-permute-start | bytes 49160 | tf_op jit(solution)/shard_map/while/body/eval_jaxpr/ppermute | solution.py:9
  57.6 5.6 %collective-permute-start.1 = (bf16[8,8,128]{2,0,1:T(8,128)(2,1)S(1)}, bf16[8,8,128]{2,0,1:T(8,128)(2,1)S(1)}, u32[]{:S(2)}, u32[]{:S(2)}) collective-permute-start(bf16[8,8,128]{2,0,1:T(8,128)(2,1)S(1)} %copy.77), channel_id=1, source_target_pairs={{0,4},{4,8},{8,12},{12,16},{16,20},{20,24},{24,28},{28,0},{1,5},{5... | collective-permute-start | bytes 49160 | tf_op jit(solution)/shard_map/while/body/eval_jaxpr/ppermute | solution.py:9
  57.7 5.4 %collective-permute-start.2 = (f32[8,8]{1,0:T(8,128)S(1)}, f32[8,8]{1,0:T(8,128)S(1)}, u32[]{:S(2)}, u32[]{:S(2)}) collective-permute-start(f32[8,8]{1,0:T(8,128)S(1)} %copy.78), channel_id=1, source_target_pairs={{0,4},{4,8},{8,12},{12,16},{16,20},{20,24},{24,28},{28,0},{1,5},{5... | collective-permute-start | bytes 776 | tf_op jit(solution)/shard_map/while/body/eval_jaxpr/ppermute | solution.py:9
  57.7 5.4 %collective-permute-start.3 = (f32[8,8]{1,0:T(8,128)S(1)}, f32[8,8]{1,0:T(8,128)S(1)}, u32[]{:S(2)}, u32[]{:S(2)}) collective-permute-start(f32[8,8]{1,0:T(8,128)S(1)} %copy.79), channel_id=1, source_target_pairs={{0,4},{4,8},{8,12},{12,16},{16,20},{20,24},{24,28},{28,0},{1,5},{5... | collective-permute-start | bytes 776 | tf_op jit(solution)/shard_map/while/body/eval_jaxpr/ppermute | solution.py:9
  61.0 1.0 copy-start.1
  62.3 4.3 %collective-permute-start.4 = (f32[8,8,128]{2,1,0:T(8,128)S(1)}, f32[8,8,128]{2,1,0:T(8,128)S(1)}, u32[]{:S(2)}, u32[]{:S(2)}) collective-permute-start(f32[8,8,128]{2,1,0:T(8,128)S(1)} %fusion.72), channel_id=1, source_target_pairs={{0,4},{4,8},{8,12},{12,16},{16,20},{20,24},{24,28},{28,0},{1,5},{5... | collective-permute-start | bytes 98312 | tf_op jit(solution)/shard_map/while/body/eval_jaxpr/ppermute | solution.py:9
  66.6 4.5 %collective-permute-start = (bf16[8,8,128]{2,0,1:T(8,128)(2,1)S(1)}, bf16[8,8,128]{2,0,1:T(8,128)(2,1)S(1)}, u32[]{:S(2)}, u32[]{:S(2)}) collective-permute-start(bf16[8,8,128]{2,0,1:T(8,128)(2,1)S(1)} %copy.76), channel_id=1, source_target_pairs={{0,4},{4,8},{8,12},{12,16},{16,20},{20,24},{24,28},{28,0},{1,5},{5... | collective-permute-start | bytes 49160 | tf_op jit(solution)/shard_map/while/body/eval_jaxpr/ppermute | solution.py:9
  66.6 4.5 %collective-permute-start.1 = (bf16[8,8,128]{2,0,1:T(8,128)(2,1)S(1)}, bf16[8,8,128]{2,0,1:T(8,128)(2,1)S(1)}, u32[]{:S(2)}, u32[]{:S(2)}) collective-permute-start(bf16[8,8,128]{2,0,1:T(8,128)(2,1)S(1)} %copy.77), channel_id=1, source_target_pairs={{0,4},{4,8},{8,12},{12,16},{16,20},{20,24},{24,28},{28,0},{1,5},{5... | collective-permute-start | bytes 49160 | tf_op jit(solution)/shard_map/while/body/eval_jaxpr/ppermute | solution.py:9
  66.7 4.4 %collective-permute-start.2 = (f32[8,8]{1,0:T(8,128)S(1)}, f32[8,8]{1,0:T(8,128)S(1)}, u32[]{:S(2)}, u32[]{:S(2)}) collective-permute-start(f32[8,8]{1,0:T(8,128)S(1)} %copy.78), channel_id=1, source_target_pairs={{0,4},{4,8},{8,12},{12,16},{16,20},{20,24},{24,28},{28,0},{1,5},{5... | collective-permute-start | bytes 776 | tf_op jit(solution)/shard_map/while/body/eval_jaxpr/ppermute | solution.py:9
  66.8 4.4 %collective-permute-start.3 = (f32[8,8]{1,0:T(8,128)S(1)}, f32[8,8]{1,0:T(8,128)S(1)}, u32[]{:S(2)}, u32[]{:S(2)}) collective-permute-start(f32[8,8]{1,0:T(8,128)S(1)} %copy.79), channel_id=1, source_target_pairs={{0,4},{4,8},{8,12},{12,16},{16,20},{20,24},{24,28},{28,0},{1,5},{5... | collective-permute-start | bytes 776 | tf_op jit(solution)/shard_map/while/body/eval_jaxpr/ppermute | solution.py:9
  69.0 1.0 copy-start.1
  70.3 4.3 %collective-permute-start.4 = (f32[8,8,128]{2,1,0:T(8,128)S(1)}, f32[8,8,128]{2,1,0:T(8,128)S(1)}, u32[]{:S(2)}, u32[]{:S(2)}) collective-permute-start(f32[8,8,128]{2,1,0:T(8,128)S(1)} %fusion.72), channel_id=1, source_target_pairs={{0,4},{4,8},{8,12},{12,16},{16,20},{20,24},{24,28},{28,0},{1,5},{5... | collective-permute-start | bytes 98312 | tf_op jit(solution)/shard_map/while/body/eval_jaxpr/ppermute | solution.py:9
  74.6 5.6 %collective-permute-start = (bf16[8,8,128]{2,0,1:T(8,128)(2,1)S(1)}, bf16[8,8,128]{2,0,1:T(8,128)(2,1)S(1)}, u32[]{:S(2)}, u32[]{:S(2)}) collective-permute-start(bf16[8,8,128]{2,0,1:T(8,128)(2,1)S(1)} %copy.76), channel_id=1, source_target_pairs={{0,4},{4,8},{8,12},{12,16},{16,20},{20,24},{24,28},{28,0},{1,5},{5... | collective-permute-start | bytes 49160 | tf_op jit(solution)/shard_map/while/body/eval_jaxpr/ppermute | solution.py:9
  74.6 5.6 %collective-permute-start.1 = (bf16[8,8,128]{2,0,1:T(8,128)(2,1)S(1)}, bf16[8,8,128]{2,0,1:T(8,128)(2,1)S(1)}, u32[]{:S(2)}, u32[]{:S(2)}) collective-permute-start(bf16[8,8,128]{2,0,1:T(8,128)(2,1)S(1)} %copy.77), channel_id=1, source_target_pairs={{0,4},{4,8},{8,12},{12,16},{16,20},{20,24},{24,28},{28,0},{1,5},{5... | collective-permute-start | bytes 49160 | tf_op jit(solution)/shard_map/while/body/eval_jaxpr/ppermute | solution.py:9
  74.7 5.4 %collective-permute-start.2 = (f32[8,8]{1,0:T(8,128)S(1)}, f32[8,8]{1,0:T(8,128)S(1)}, u32[]{:S(2)}, u32[]{:S(2)}) collective-permute-start(f32[8,8]{1,0:T(8,128)S(1)} %copy.78), channel_id=1, source_target_pairs={{0,4},{4,8},{8,12},{12,16},{16,20},{20,24},{24,28},{28,0},{1,5},{5... | collective-permute-start | bytes 776 | tf_op jit(solution)/shard_map/while/body/eval_jaxpr/ppermute | solution.py:9
  74.8 5.4 %collective-permute-start.3 = (f32[8,8]{1,0:T(8,128)S(1)}, f32[8,8]{1,0:T(8,128)S(1)}, u32[]{:S(2)}, u32[]{:S(2)}) collective-permute-start(f32[8,8]{1,0:T(8,128)S(1)} %copy.79), channel_id=1, source_target_pairs={{0,4},{4,8},{8,12},{12,16},{16,20},{20,24},{24,28},{28,0},{1,5},{5... | collective-permute-start | bytes 776 | tf_op jit(solution)/shard_map/while/body/eval_jaxpr/ppermute | solution.py:9
  79.4 4.3 %collective-permute-start.4 = (f32[8,8,128]{2,1,0:T(8,128)S(1)}, f32[8,8,128]{2,1,0:T(8,128)S(1)}, u32[]{:S(2)}, u32[]{:S(2)}) collective-permute-start(f32[8,8,128]{2,1,0:T(8,128)S(1)} %fusion.72), channel_id=1, source_target_pairs={{0,4},{4,8},{8,12},{12,16},{16,20},{20,24},{24,28},{28,0},{1,5},{5... | collective-permute-start | bytes 98312 | tf_op jit(solution)/shard_map/while/body/eval_jaxpr/ppermute | solution.py:9
  83.6 4.5 %collective-permute-start = (bf16[8,8,128]{2,0,1:T(8,128)(2,1)S(1)}, bf16[8,8,128]{2,0,1:T(8,128)(2,1)S(1)}, u32[]{:S(2)}, u32[]{:S(2)}) collective-permute-start(bf16[8,8,128]{2,0,1:T(8,128)(2,1)S(1)} %copy.76), channel_id=1, source_target_pairs={{0,4},{4,8},{8,12},{12,16},{16,20},{20,24},{24,28},{28,0},{1,5},{5... | collective-permute-start | bytes 49160 | tf_op jit(solution)/shard_map/while/body/eval_jaxpr/ppermute | solution.py:9
  83.7 4.5 %collective-permute-start.1 = (bf16[8,8,128]{2,0,1:T(8,128)(2,1)S(1)}, bf16[8,8,128]{2,0,1:T(8,128)(2,1)S(1)}, u32[]{:S(2)}, u32[]{:S(2)}) collective-permute-start(bf16[8,8,128]{2,0,1:T(8,128)(2,1)S(1)} %copy.77), channel_id=1, source_target_pairs={{0,4},{4,8},{8,12},{12,16},{16,20},{20,24},{24,28},{28,0},{1,5},{5... | collective-permute-start | bytes 49160 | tf_op jit(solution)/shard_map/while/body/eval_jaxpr/ppermute | solution.py:9
  83.7 4.4 %collective-permute-start.2 = (f32[8,8]{1,0:T(8,128)S(1)}, f32[8,8]{1,0:T(8,128)S(1)}, u32[]{:S(2)}, u32[]{:S(2)}) collective-permute-start(f32[8,8]{1,0:T(8,128)S(1)} %copy.78), channel_id=1, source_target_pairs={{0,4},{4,8},{8,12},{12,16},{16,20},{20,24},{24,28},{28,0},{1,5},{5... | collective-permute-start | bytes 776 | tf_op jit(solution)/shard_map/while/body/eval_jaxpr/ppermute | solution.py:9
  83.8 4.4 %collective-permute-start.3 = (f32[8,8]{1,0:T(8,128)S(1)}, f32[8,8]{1,0:T(8,128)S(1)}, u32[]{:S(2)}, u32[]{:S(2)}) collective-permute-start(f32[8,8]{1,0:T(8,128)S(1)} %copy.79), channel_id=1, source_target_pairs={{0,4},{4,8},{8,12},{12,16},{16,20},{20,24},{24,28},{28,0},{1,5},{5... | collective-permute-start | bytes 776 | tf_op jit(solution)/shard_map/while/body/eval_jaxpr/ppermute | solution.py:9
  86.0 1.0 copy-start.1
  87.4 4.3 %collective-permute-start.4 = (f32[8,8,128]{2,1,0:T(8,128)S(1)}, f32[8,8,128]{2,1,0:T(8,128)S(1)}, u32[]{:S(2)}, u32[]{:S(2)}) collective-permute-start(f32[8,8,128]{2,1,0:T(8,128)S(1)} %fusion.72), channel_id=1, source_target_pairs={{0,4},{4,8},{8,12},{12,16},{16,20},{20,24},{24,28},{28,0},{1,5},{5... | collective-permute-start | bytes 98312 | tf_op jit(solution)/shard_map/while/body/eval_jaxpr/ppermute | solution.py:9
  91.7 5.6 %collective-permute-start = (bf16[8,8,128]{2,0,1:T(8,128)(2,1)S(1)}, bf16[8,8,128]{2,0,1:T(8,128)(2,1)S(1)}, u32[]{:S(2)}, u32[]{:S(2)}) collective-permute-start(bf16[8,8,128]{2,0,1:T(8,128)(2,1)S(1)} %copy.76), channel_id=1, source_target_pairs={{0,4},{4,8},{8,12},{12,16},{16,20},{20,24},{24,28},{28,0},{1,5},{5... | collective-permute-start | bytes 49160 | tf_op jit(solution)/shard_map/while/body/eval_jaxpr/ppermute | solution.py:9
  91.7 5.6 %collective-permute-start.1 = (bf16[8,8,128]{2,0,1:T(8,128)(2,1)S(1)}, bf16[8,8,128]{2,0,1:T(8,128)(2,1)S(1)}, u32[]{:S(2)}, u32[]{:S(2)}) collective-permute-start(bf16[8,8,128]{2,0,1:T(8,128)(2,1)S(1)} %copy.77), channel_id=1, source_target_pairs={{0,4},{4,8},{8,12},{12,16},{16,20},{20,24},{24,28},{28,0},{1,5},{5... | collective-permute-start | bytes 49160 | tf_op jit(solution)/shard_map/while/body/eval_jaxpr/ppermute | solution.py:9
  91.7 5.4 %collective-permute-start.2 = (f32[8,8]{1,0:T(8,128)S(1)}, f32[8,8]{1,0:T(8,128)S(1)}, u32[]{:S(2)}, u32[]{:S(2)}) collective-permute-start(f32[8,8]{1,0:T(8,128)S(1)} %copy.78), channel_id=1, source_target_pairs={{0,4},{4,8},{8,12},{12,16},{16,20},{20,24},{24,28},{28,0},{1,5},{5... | collective-permute-start | bytes 776 | tf_op jit(solution)/shard_map/while/body/eval_jaxpr/ppermute | solution.py:9
  91.8 5.4 %collective-permute-start.3 = (f32[8,8]{1,0:T(8,128)S(1)}, f32[8,8]{1,0:T(8,128)S(1)}, u32[]{:S(2)}, u32[]{:S(2)}) collective-permute-start(f32[8,8]{1,0:T(8,128)S(1)} %copy.79), channel_id=1, source_target_pairs={{0,4},{4,8},{8,12},{12,16},{16,20},{20,24},{24,28},{28,0},{1,5},{5... | collective-permute-start | bytes 776 | tf_op jit(solution)/shard_map/while/body/eval_jaxpr/ppermute | solution.py:9
  96.4 4.3 %collective-permute-start.4 = (f32[8,8,128]{2,1,0:T(8,128)S(1)}, f32[8,8,128]{2,1,0:T(8,128)S(1)}, u32[]{:S(2)}, u32[]{:S(2)}) collective-permute-start(f32[8,8,128]{2,1,0:T(8,128)S(1)} %fusion.72), channel_id=1, source_target_pairs={{0,4},{4,8},{8,12},{12,16},{16,20},{20,24},{24,28},{28,0},{1,5},{5... | collective-permute-start | bytes 98312 | tf_op jit(solution)/shard_map/while/body/eval_jaxpr/ppermute | solution.py:9
  102.0 4.2 %collective-permute-start.5 = (bf16[8,8,128]{2,1,0:T(8,128)(2,1)S(1)}, bf16[8,8,128]{2,1,0:T(8,128)(2,1)}, u32[]{:S(2)}, u32[]{:S(2)}) collective-permute-start(bf16[8,8,128]{2,1,0:T(8,128)(2,1)S(1)} %fusion.32), channel_id=1, source_target_pairs={{0,4},{4,8},{8,12},{12,16},{16,20},{20,24},{24,28},{28,0},{1,5},{5... | collective-permute-start | bytes 49160 | tf_op jit(solution)/shard_map/ppermute | solution.py:9
  106.3 8.8 %all-to-all-start.4 = ((bf16[8,8,128]{2,1,0:T(8,128)(2,1)}), bf16[8,8,128]{2,1,0:T(8,128)(2,1)S(1)}, u32[]{:S(2)}, u32[]{:S(2)}) async-start(bf16[8,8,128]{2,1,0:T(8,128)(2,1)} %collective-permute-done.5), calls=%async_computation.4 | async-start | bytes 32768 | tf_op jit(solution)/shard_map/all_to_all | solution.py:104
  (4 other events, 3.5 us)
